TPU v7x, 32 devices: a whole 2x2x4 slice. The times are simulated.
32 devices in a mesh: row: 8 (over y, x, core), col: 4 (over z).
Axes of the slice: x: 2, y: 2, z: 4, core: 2. Of those that a mesh axis runs over, the one named last changes fastest.
Arguments:
- history: float32 [3, 512, 4096], P(None, None, ('row', 'col')), may hold values from -8 to 8
Outputs:
- orbitals: float32 [512, 4096], P(None, ('row', 'col'))
All inputs are finite; a program needn't handle non-finite values.
Results may differ from a plain program's by a relative error of at most 0.0003.
Values sent between devices are 32-bit elements; how exact they have to be, the bound alone decides.
A program may use at most 64 MiB of HBM per device.

v0:
```python
import jax
import jax.numpy as jnp
from jax import lax
from jax.sharding import PartitionSpec as P


def on_device(history):
    precise = lax.Precision.HIGHEST
    npw_total = history.shape[2] * lax.axis_size("row") * lax.axis_size("col")
    newest = history[0]
    local_terms = tuple(
        (jnp.einsum("ip,jp->ij", newest, history[index], precision=precise) for index in range(3))
    )
    summed = lax.psum(local_terms, ("row", "col"))
    weights = (2.5, -2.0, 0.5)
    predicted = jnp.zeros(newest.shape, jnp.float32)
    for index in range(3):
        project = summed[index] / npw_total
        predicted = predicted + weights[index] * jnp.dot(project, history[index], precision=precise)
    local_gram = jnp.einsum("ip,jp->ij", predicted, predicted, precision=precise)
    gram = lax.psum(local_gram, ("row", "col"))
    factor = jnp.linalg.cholesky(gram / npw_total)
    return lax.linalg.triangular_solve(factor, predicted, left_side=True, lower=True)


def solution(mesh):
    return jax.shard_map(
        on_device,
        mesh=mesh,
        in_specs=(P(None, None, ("row", "col")),),
        out_specs=P(None, ("row", "col")),
        check_vma=False,
    )
```

profile of v0, /device:TPU:0, one launch (start us, length us, event | category | flops | bytes accessed | tf_op | source)
XLA Modules:
  0.0 441.3 jit_solution(1607792850113480831)
XLA Ops:
  6.5 0.0 copy-start
  6.5 0.0 all-reduce.7.cloned.1.call-start
  6.5 3.1 fusion.11
  9.7 0.0 copy-done
  9.7 2.0 fusion.14
  11.6 2.0 fusion.19
  13.6 0.0 all-reduce.7.cloned.1.call-update
  13.6 0.5 all-reduce.5.cloned.1.call-start
  14.1 141.3 %all-reduce.7.cloned.1.call-done = (f32[512,512]{0,1:T(8,128)}, f32[512,512]{0,1:T(8,128)}, f32[512,512]{0,1:T(8,128)}) async-done(((f32[512,512]{0,1:T(8,128)}, f32[512,512]{0,1:T(8,128)}, f32[512,512]{0,1:T(8,128)}), (f32[512,512]{0,1:T(8,128)}, f32[512,512]{0,1:T(8,128)}, f32[512,512]{0,1:T(8,128)})) %all-reduce.7.cloned.1.call-update) | async-done | bytes 3145744 | tf_op jit(solution)/shard_map/psum | solution.py:14
  155.4 0.0 copy-start.3
  155.4 3.1 convolution_multiply_fusion.2
  158.5 0.0 copy-start.2
  158.6 0.0 copy-done.3
  158.6 1.8 fusion.1
  160.4 0.0 copy-done.2
  160.4 1.8 fusion
  162.2 2.0 fusion.61
  164.3 0.0 all-reduce.5.cloned.1.call-update
  164.3 130.2 %all-reduce.5.cloned.1.call-done = f32[512,512]{0,1:T(8,128)} async-done(((f32[512,512]{0,1:T(8,128)}), f32[512,512]{0,1:T(8,128)}) %all-reduce.5.cloned.1.call-update) | async-done | bytes 1048592 | tf_op jit(solution)/shard_map/psum | solution.py:21
  294.5 1.3 broadcast_multiply_fusion
  295.8 0.0 copy-start.1
  295.8 0.3 copy.3
  296.2 0.9 copy-done.1
  297.0 0.2 fusion.2
  297.3 11.7 %cholesky.104 = f32[128,128]{1,0:T(8,128)S(1)} custom-call(f32[128,128]{1,0:T(8,128)S(1)} %cholesky.266), custom_call_target="Cholesky" | custom-call | tf_op jit(solution)/shard_map/jit(cholesky)/cholesky | solution.py:22
  309.0 10.0 %custom-call.30 = f32[1,128,128]{1,2,0:T(8,128)S(1)} custom-call(f32[1,128,128]{2,1,0:T(8,128)S(1)} %get-tuple-element.35), custom_call_target="InvertDiagBlocksLowerTriangular" | custom-call | tf_op jit(solution)/shard_map/jit(cholesky)/cholesky | solution.py:22
  319.0 0.1 cholesky.224
  319.1 0.3 constant_dynamic-update-slice_fusion.3
  319.4 0.3 convolution_subtract_fusion
  319.8 11.7 %cholesky.217 = f32[128,128]{1,0:T(8,128)S(1)} custom-call(f32[128,128]{1,0:T(8,128)S(1)} %cholesky.270), custom_call_target="Cholesky" | custom-call | tf_op jit(solution)/shard_map/jit(cholesky)/cholesky | solution.py:22
  331.5 9.8 %custom-call.31 = f32[1,128,128]{1,2,0:T(8,128)S(1)} custom-call(f32[1,128,128]{2,1,0:T(8,128)S(1)} %get-tuple-element.32), custom_call_target="InvertDiagBlocksLowerTriangular" | custom-call | tf_op jit(solution)/shard_map/jit(cholesky)/cholesky | solution.py:22
  341.4 0.3 convolution_dynamic-update-slice_fusion
  341.6 0.4 convolution_subtract_fusion.1
  342.0 11.7 %cholesky.238 = f32[128,128]{1,0:T(8,128)S(1)} custom-call(f32[128,128]{1,0:T(8,128)S(1)} %cholesky.275), custom_call_target="Cholesky" | custom-call | tf_op jit(solution)/shard_map/jit(cholesky)/cholesky | solution.py:22
  353.8 0.7 compare_reduce_fusion.1
  354.5 10.0 %custom-call.32 = f32[1,128,128]{1,2,0:T(8,128)S(1)} custom-call(f32[1,128,128]{2,1,0:T(8,128)S(1)} %get-tuple-element.29), custom_call_target="InvertDiagBlocksLowerTriangular" | custom-call | tf_op jit(solution)/shard_map/jit(cholesky)/cholesky | solution.py:22
  364.5 0.2 convolution_dynamic-update-slice_fusion.1
  364.7 0.4 convolution_subtract_fusion.5
  365.1 11.7 %cholesky.255 = f32[128,128]{1,0:T(8,128)S(1)} custom-call(f32[128,128]{1,0:T(8,128)S(1)} %convolution_subtract_fusion.5), custom_call_target="Cholesky" | custom-call | tf_op jit(solution)/shard_map/jit(cholesky)/cholesky | solution.py:22
  376.8 0.6 compare_reduce_fusion
  377.5 0.7 compare_reduce_fusion.2
  380.7 0.1 select_select_fusion
  380.8 10.6 %while.1 = (s32[]{:T(128)}, f32[512,512]{1,0:T(8,128)S(1)}, s32[4,2]{0,1:T(2,128)S(1)}, f32[4,128,128]{2,1,0:T(8,128)}, s32[]{:T(128)}) while((s32[]{:T(128)}, f32[512,512]{1,0:T(8,128)S(1)}, s32[4,2]{0,1:T(2,128)S(1)}, f32[4,128,128]{2,1,0:T(8,128)}, s32[]{:T(128)}) %tuple.27), condition=%wide.while_cond, body=%wide.while_body.sunk | while | flops 2 | bytes 132705 | solution.py:23
  380.9 0.1 constant_dynamic-slice_fusion.2
  380.9 0.6 fusion.70
  381.5 2.0 bitcast_dynamic-update-slice_fusion.2
  383.5 0.1 constant_dynamic-slice_fusion.2
  383.6 0.6 fusion.70
  384.2 2.0 bitcast_dynamic-update-slice_fusion.2
  386.2 0.1 constant_dynamic-slice_fusion.2
  386.2 0.6 fusion.70
  386.8 2.0 bitcast_dynamic-update-slice_fusion.2
  388.8 0.1 constant_dynamic-slice_fusion.2
  388.9 0.6 fusion.70
  389.5 2.0 bitcast_dynamic-update-slice_fusion.2
  391.4 40.1 %custom-call.33 = f32[4,128,128]{1,2,0:T(8,128)S(1)} custom-call(f32[4,128,128]{2,1,0:T(8,128)} %get-tuple-element.12), custom_call_target="InvertDiagBlocksLowerTriangular" | custom-call | tf_op jit(solution)/shard_map/triangular_solve | solution.py:23
  431.6 0.3 fusion.48
  431.9 0.2 convolution_subtract_fusion.3
  432.1 0.3 fusion.47
  432.4 0.3 convolution_subtract_fusion.2
  432.6 0.3 fusion.45
  432.9 0.3 convolution_subtract_fusion.4
  433.3 0.3 fusion.44
  433.5 0.7 pad_maximum_fusion
  (10 shorter events, 0.2 us)
Async XLA Ops:
  6.5 3.1 copy-start
  6.5 148.9 %all-reduce.7.cloned.1.call-start = ((), (), s32[]{:S(2)}) async-start(), calls=%async_computation.1 | async-start | bytes 6291456 | tf_op jit(solution)/shard_map/psum | solution.py:14
  13.6 280.9 %all-reduce.5.cloned.1.call-start = ((), (), s32[]{:S(2)}) async-start(), calls=%async_computation | async-start | bytes 2097152 | tf_op jit(solution)/shard_map/psum | solution.py:21
  155.4 3.1 copy-start.3
  158.5 1.8 copy-start.2
  295.8 1.2 copy-start.1
Sparse Core Ops, SparseCore 0:
  13.8 141.6 all-reduce.6
  164.4 130.0 all-reduce.4
where the time goes:
time: 444 us; the launch traced here: 441 us
  waiting for transfers between devices  271 us (61%)
  other arithmetic  121 us (27%)
  matrix products  19.7 us (4%)
  between operations  16.4 us (4%)
  local copies, waits for them, and re-layouts  11.9 us (3%)
    psum x1, waiting for transfers between devices, on_device(): summed = lax.psum(local_terms, ('row', 'col'))  141 us
    psum x1, waiting for transfers between devices, on_device(): gram = lax.psum(local_gram, ('row', 'col'))  130 us
    another operation x14, other arithmetic, on_device(): factor = jnp.linalg.cholesky(gram / npw_total)  78.8 us
    another operation x4, other arithmetic, on_device(): lax.linalg.triangular_solve(factor, predicted, left_side=True, lower=True)  41 us
    another operation x12, local copies, waits for them, and re-layouts  10.6 us
  transfers between devices with their start and end apart: 2, of which 2 were waited for; matrix products, arithmetic and copies ran while one was open for 0% of the time, Pallas kernels for 0%

commit v1 on v0

--- a/solution.py
+++ b/solution.py
@@ -11,7 +11,7 @@
     local_terms = tuple(
         (jnp.einsum("ip,jp->ij", newest, history[index], precision=precise) for index in range(3))
     )
-    summed = lax.psum(local_terms, ("row", "col"))
+    summed = lax.psum(lax.psum(local_terms, "row"), "col")
     weights = (2.5, -2.0, 0.5)
     predicted = jnp.zeros(newest.shape, jnp.float32)
     for index in range(3):

time: 444 us -> 498 us (1.12)
  waiting for transfers between devices: 271 us -> 325 us
    psum x1 -> x2, waiting for transfers between devices: 141 us -> 196 us  [on_device(): summed = lax.psum(lax.psum(local_terms, 'row'), 'col')]
  transfers between devices with their start and end apart: 2 -> 3, of which waited for: 2 -> 3; matrix products, arithmetic and copies ran while one was open for 0% -> 0% of each run, Pallas kernels for 0% -> 0%
where the time goes in v1:
time: 498 us; the launch traced here: 495 us
  waiting for transfers between devices  325 us (65%)
  other arithmetic  121 us (24%)
  matrix products  19.7 us (4%)
  between operations  16.1 us (3%)
  local copies, waits for them, and re-layouts  11.9 us (2%)
    psum x2, waiting for transfers between devices, on_device(): summed = lax.psum(lax.psum(local_terms, 'row'), 'col')  196 us
    psum x1, waiting for transfers between devices, on_device(): gram = lax.psum(local_gram, ('row', 'col'))  130 us
    another operation x14, other arithmetic, on_device(): factor = jnp.linalg.cholesky(gram / npw_total)  78.8 us
    another operation x4, other arithmetic, on_device(): lax.linalg.triangular_solve(factor, predicted, left_side=True, lower=True)  41 us
    another operation x12, local copies, waits for them, and re-layouts  10.6 us
  transfers between devices with their start and end apart: 3, of which 3 were waited for; matrix products, arithmetic and copies ran while one was open for 0% of the time, Pallas kernels for 0%

profile of v1, /device:TPU:0, one launch (start us, length us, event | category | flops | bytes accessed | tf_op | source)
XLA Modules:
  0.0 495.0 jit_solution(17054735589472089027)
XLA Ops:
  6.5 0.0 all-reduce.9.cloned.1.call-start
  6.5 3.1 fusion.11
  9.7 0.0 copy-done
  9.7 2.0 fusion.14
  11.6 2.0 fusion.19
  13.6 0.0 all-reduce.9.cloned.1.call-update
  13.6 0.0 all-reduce.11.cloned.1.call-start
  13.7 72.3 %all-reduce.9.cloned.1.call-done = (f32[512,512]{0,1:T(8,128)}, f32[512,512]{0,1:T(8,128)}, f32[512,512]{0,1:T(8,128)}) async-done(((f32[512,512]{0,1:T(8,128)}, f32[512,512]{0,1:T(8,128)}, f32[512,512]{0,1:T(8,128)}), (f32[512,512]{0,1:T(8,128)}, f32[512,512]{0,1:T(8,128)}, f32[512,512]{0,1:T(8,128)})) %all-reduce.9.cloned.1.call-update) | async-done | bytes 3145744 | tf_op jit(solution)/shard_map/psum | solution.py:14
  86.0 0.0 all-reduce.11.cloned.1.call-update
  86.0 0.5 all-reduce.7.cloned.1.call-start
  86.5 123.2 %all-reduce.11.cloned.1.call-done = (f32[512,512]{0,1:T(8,128)}, f32[512,512]{0,1:T(8,128)}, f32[512,512]{0,1:T(8,128)}) async-done(((f32[512,512]{0,1:T(8,128)}, f32[512,512]{0,1:T(8,128)}, f32[512,512]{0,1:T(8,128)}), (f32[512,512]{0,1:T(8,128)}, f32[512,512]{0,1:T(8,128)}, f32[512,512]{0,1:T(8,128)})) %all-reduce.11.cloned.1.call-update) | async-done | bytes 3145744 | tf_op jit(solution)/shard_map/psum | solution.py:14
  209.7 3.1 convolution_multiply_fusion.2
  212.9 0.0 copy-start.2
  212.9 0.0 copy-done.3
  212.9 1.8 fusion.1
  214.7 0.0 copy-done.2
  214.7 1.8 fusion
  216.6 2.0 fusion.61
  218.6 0.0 all-reduce.7.cloned.1.call-update
  218.6 129.9 %all-reduce.7.cloned.1.call-done = f32[512,512]{0,1:T(8,128)} async-done(((f32[512,512]{0,1:T(8,128)}), f32[512,512]{0,1:T(8,128)}) %all-reduce.7.cloned.1.call-update) | async-done | bytes 1048592 | tf_op jit(solution)/shard_map/psum | solution.py:21
  348.5 1.3 broadcast_multiply_fusion
  349.8 0.3 copy.3
  350.2 0.9 copy-done.1
  351.0 0.2 fusion.2
  351.3 11.7 %cholesky.104 = f32[128,128]{1,0:T(8,128)S(1)} custom-call(f32[128,128]{1,0:T(8,128)S(1)} %cholesky.266), custom_call_target="Cholesky" | custom-call | tf_op jit(solution)/shard_map/jit(cholesky)/cholesky | solution.py:22
  363.1 10.0 %custom-call.30 = f32[1,128,128]{1,2,0:T(8,128)S(1)} custom-call(f32[1,128,128]{2,1,0:T(8,128)S(1)} %get-tuple-element.38), custom_call_target="InvertDiagBlocksLowerTriangular" | custom-call | tf_op jit(solution)/shard_map/jit(cholesky)/cholesky | solution.py:22
  373.0 0.1 cholesky.224
  373.1 0.3 constant_dynamic-update-slice_fusion.3
  373.5 0.3 convolution_subtract_fusion
  373.8 11.7 %cholesky.217 = f32[128,128]{1,0:T(8,128)S(1)} custom-call(f32[128,128]{1,0:T(8,128)S(1)} %cholesky.270), custom_call_target="Cholesky" | custom-call | tf_op jit(solution)/shard_map/jit(cholesky)/cholesky | solution.py:22
  385.6 9.8 %custom-call.31 = f32[1,128,128]{1,2,0:T(8,128)S(1)} custom-call(f32[1,128,128]{2,1,0:T(8,128)S(1)} %get-tuple-element.35), custom_call_target="InvertDiagBlocksLowerTriangular" | custom-call | tf_op jit(solution)/shard_map/jit(cholesky)/cholesky | solution.py:22
  395.4 0.3 convolution_dynamic-update-slice_fusion
  395.6 0.4 convolution_subtract_fusion.1
  396.1 11.7 %cholesky.238 = f32[128,128]{1,0:T(8,128)S(1)} custom-call(f32[128,128]{1,0:T(8,128)S(1)} %cholesky.275), custom_call_target="Cholesky" | custom-call | tf_op jit(solution)/shard_map/jit(cholesky)/cholesky | solution.py:22
  407.8 0.7 compare_reduce_fusion.1
  408.5 10.0 %custom-call.32 = f32[1,128,128]{1,2,0:T(8,128)S(1)} custom-call(f32[1,128,128]{2,1,0:T(8,128)S(1)} %get-tuple-element.32), custom_call_target="InvertDiagBlocksLowerTriangular" | custom-call | tf_op jit(solution)/shard_map/jit(cholesky)/cholesky | solution.py:22
  418.5 0.2 convolution_dynamic-update-slice_fusion.1
  418.7 0.4 convolution_subtract_fusion.5
  419.1 11.7 %cholesky.255 = f32[128,128]{1,0:T(8,128)S(1)} custom-call(f32[128,128]{1,0:T(8,128)S(1)} %convolution_subtract_fusion.5), custom_call_target="Cholesky" | custom-call | tf_op jit(solution)/shard_map/jit(cholesky)/cholesky | solution.py:22
  430.9 0.6 compare_reduce_fusion
  431.5 0.7 compare_reduce_fusion.2
  434.7 0.1 select_select_fusion
  434.9 10.6 %while.1 = (s32[]{:T(128)}, f32[512,512]{1,0:T(8,128)S(1)}, s32[4,2]{0,1:T(2,128)S(1)}, f32[4,128,128]{2,1,0:T(8,128)}, s32[]{:T(128)}) while((s32[]{:T(128)}, f32[512,512]{1,0:T(8,128)S(1)}, s32[4,2]{0,1:T(2,128)S(1)}, f32[4,128,128]{2,1,0:T(8,128)}, s32[]{:T(128)}) %tuple.27), condition=%wide.while_cond, body=%wide.while_body.sunk | while | flops 2 | bytes 132705 | solution.py:23
  434.9 0.1 constant_dynamic-slice_fusion.2
  435.0 0.6 fusion.70
  435.6 2.0 bitcast_dynamic-update-slice_fusion.2
  437.5 0.1 constant_dynamic-slice_fusion.2
  437.6 0.6 fusion.70
  438.2 2.0 bitcast_dynamic-update-slice_fusion.2
  440.2 0.1 constant_dynamic-slice_fusion.2
  440.2 0.6 fusion.70
  440.8 2.0 bitcast_dynamic-update-slice_fusion.2
  442.8 0.1 constant_dynamic-slice_fusion.2
  442.9 0.6 fusion.70
  443.5 2.0 bitcast_dynamic-update-slice_fusion.2
  445.5 40.1 %custom-call.33 = f32[4,128,128]{1,2,0:T(8,128)S(1)} custom-call(f32[4,128,128]{2,1,0:T(8,128)} %get-tuple-element.12), custom_call_target="InvertDiagBlocksLowerTriangular" | custom-call | tf_op jit(solution)/shard_map/triangular_solve | solution.py:23
  485.6 0.3 fusion.48
  485.9 0.2 convolution_subtract_fusion.3
  486.1 0.3 fusion.47
  486.4 0.3 convolution_subtract_fusion.2
  486.7 0.3 fusion.45
  487.0 0.3 convolution_subtract_fusion.4
  487.3 0.3 fusion.44
  487.6 0.7 pad_maximum_fusion
  (13 shorter events, 0.2 us)
Async XLA Ops:
  6.5 3.1 copy-start
  6.5 79.4 %all-reduce.9.cloned.1.call-start = ((), (), s32[]{:S(2)}) async-start(), calls=%async_computation.1 | async-start | bytes 6291456 | tf_op jit(solution)/shard_map/psum | solution.py:14
  13.6 196.1 %all-reduce.11.cloned.1.call-start = ((), (), s32[]{:S(2)}) async-start(), calls=%async_computation.2 | async-start | bytes 6291456 | tf_op jit(solution)/shard_map/psum | solution.py:14
  86.0 262.5 %all-reduce.7.cloned.1.call-start = ((), (), s32[]{:S(2)}) async-start(), calls=%async_computation | async-start | bytes 2097152 | tf_op jit(solution)/shard_map/psum | solution.py:21
  209.7 3.1 copy-start.3
  212.9 1.9 copy-start.2
  349.8 1.2 copy-start.1
Sparse Core Ops, SparseCore 0:
  13.8 72.1 all-reduce.8
  88.5 121.1 all-reduce.10
  218.7 129.7 all-reduce.6
